TPU v7x, 512 devices: a whole 4x8x8 slice. The times are simulated.
512 devices in a mesh: inst: 64 (over z, x, core), tp: 8 (over y).
Axes of the slice: x: 4, y: 8, z: 8, core: 2. Of those that a mesh axis runs over, the one named last changes fastest.
Arguments:
- queries: bfloat16 [64, 4096], P('inst', 'tp'), may hold values from -360 to 360
- slot_request: int32 [64], P('inst'), may hold values from -1 to 31, as said below
- key_cache_pages: bfloat16 [2048, 128, 1024], P('inst', None, 'tp'), may hold values from -6 to 6
- value_cache_pages: bfloat16 [2048, 128, 1024], P('inst', None, 'tp'), may hold values from -6 to 6
- page_owner: int32 [2048], P('inst'), may hold values from -1 to 31, as said below
- page_fill: int32 [2048], P('inst'), may hold values from 1 to 128
- out_weight: bfloat16 [4096, 4096], P('tp', 'inst'), may hold values from -0.09375 to 0.09375
Outputs:
- projected: bfloat16 [64, 4096], P('inst', 'tp')
Inputs may be any that keep to these rules, and one draw needn't show every extreme that they name: `slot_request`: each request id appears in exactly one slot; every other slot holds -1. `page_owner`: each entry is -1 (a free page) or a request id; every request owns at least one page.
All inputs are finite; a program needn't handle non-finite values.
Results may differ from a plain program's by a relative error of at most 0.005.
Values may be sent and summed in bfloat16 or wider, within the bound.
No kernel may reach another device: no remote copies, remote signals or barrier semaphores. Data moves between devices by JAX's collectives and lax.ppermute only.
A program may use at most 64 MiB of HBM per device.

v0:
```python
import jax
import jax.numpy as jnp
from jax import lax
from jax.sharding import PartitionSpec as P

HEAD_SIZE = 128


NEG_FILL = -1e30


def sent_to_all(x, axis):
    length = lax.axis_size(axis)
    return lax.all_to_all(jnp.broadcast_to(x[None], (length, *x.shape)), axis, 0, 0, tiled=True)


def in_order(parts, dim):
    parts = jnp.moveaxis(parts, 0, dim)
    dims = parts.shape
    return parts.reshape(*dims[:dim], dims[dim] * dims[dim + 1], *dims[dim + 2 :])


def collect(x, axis, dim):
    parts = sent_to_all(x, axis)
    return in_order(parts, dim)


def taken_together(x, axis):
    everything = sent_to_all(x, axis)
    return jnp.max(everything, axis=0)


def split_up(x, dim, length):
    before, after = (x.shape[:dim], x.shape[dim + 1 :])
    return jnp.moveaxis(x.reshape(*before, length, -1, *after), dim, 0)


def summed_on_arrival(x, axis, dim):
    parts = split_up(x, dim, lax.axis_size(axis))
    arrived = lax.all_to_all(parts, axis, split_axis=0, concat_axis=0, tiled=True)
    return arrived.sum(axis=0)


def in_one_piece(arrays, axis, dim, along):
    both = jnp.concatenate(arrays, axis=along)
    result, at, finished = (summed_on_arrival(both, axis, dim), 0, [])
    for a in arrays:
        finished.append(lax.slice_in_dim(result, at, at + a.shape[along], axis=along))
        at += a.shape[along]
    return tuple(finished)


def on_device(
    queries, slot_request, key_cache_pages, value_cache_pages, page_owner, page_fill, out_weight
):
    whole_q, whole_req = (collect(queries, "inst", 0), collect(slot_request, "inst", 0))
    n_pages, page_len, kv_width = key_cache_pages.shape
    kv_local = kv_width // HEAD_SIZE
    q_local = whole_q.shape[1] // HEAD_SIZE
    query_group = q_local // kv_local
    n_slots = whole_q.shape[0]
    n_inst = lax.axis_size("inst")
    slots_dev = n_slots // n_inst
    owner_match = (page_owner[:, None] == whole_req[None, :]) & (whole_req[None, :] >= 0)
    selected_pages = jnp.dot(
        owner_match.astype(jnp.bfloat16), whole_q, preferred_element_type=jnp.float32
    ).astype(jnp.bfloat16)
    query_portion = selected_pages.reshape(n_pages, kv_local, query_group, HEAD_SIZE)
    key_portion = key_cache_pages.reshape(n_pages, page_len, kv_local, HEAD_SIZE)
    value_portion = value_cache_pages.reshape(n_pages, page_len, kv_local, HEAD_SIZE)
    scores = jnp.einsum(
        "pkgd,ptkd->pkgt", query_portion, key_portion, preferred_element_type=jnp.float32
    ) * HEAD_SIZE ** (-0.5)
    positions = jnp.arange(page_len, dtype=jnp.int32)
    is_valid = positions[None, None, None, :] < page_fill[:, None, None, None]
    scores = jnp.where(is_valid, scores, NEG_FILL)
    page_peak = jnp.max(scores, axis=-1)
    expo_vals = jnp.exp(scores - page_peak[..., None])
    page_total = jnp.sum(expo_vals, axis=-1).reshape(n_pages, q_local)
    prob_bf = expo_vals.astype(jnp.bfloat16)
    page_out = jnp.einsum(
        "pkgt,ptkd->pkgd", prob_bf, value_portion, preferred_element_type=jnp.float32
    )
    page_out = page_out.reshape(n_pages, q_local, HEAD_SIZE)
    page_peak = page_peak.reshape(n_pages, q_local)
    chosen = owner_match[:, :, None]
    slot_peak = jnp.max(jnp.where(chosen, page_peak[:, None, :], NEG_FILL), axis=0)
    weight = jnp.exp(jnp.where(chosen, page_peak[:, None, :] - slot_peak[None], NEG_FILL))
    slot_total = jnp.sum(weight * page_total[:, None, :], axis=0)
    slot_mix = jnp.einsum("prh,phd->rhd", weight, page_out, precision=lax.Precision.HIGHEST)
    global_peak = taken_together(slot_peak, "inst")
    factor = jnp.exp(slot_peak - global_peak)
    share_mix, share_total = in_one_piece(
        ((slot_mix * factor[..., None]).reshape(n_slots, q_local * HEAD_SIZE), slot_total * factor),
        "inst",
        0,
        1,
    )
    divisor = jnp.where(share_total > 0.0, share_total, 1.0)
    attention = (
        (share_mix.reshape(slots_dev, q_local, HEAD_SIZE) / divisor[..., None])
        .reshape(slots_dev, q_local * HEAD_SIZE)
        .astype(jnp.bfloat16)
    )
    every_row = collect(attention, "inst", 0)
    column_part = jnp.dot(every_row, out_weight, preferred_element_type=jnp.float32)
    partial_value = lax.all_to_all(column_part, "inst", split_axis=0, concat_axis=1, tiled=True)
    return summed_on_arrival(partial_value, "tp", 1).astype(jnp.bfloat16)


def solution(mesh):
    return jax.shard_map(
        on_device,
        mesh=mesh,
        in_specs=(
            P("inst", "tp"),
            P("inst"),
            P("inst", None, "tp"),
            P("inst", None, "tp"),
            P("inst"),
            P("inst"),
            P("tp", "inst"),
        ),
        out_specs=P("inst", "tp"),
        check_vma=False,
    )
```

profile of v0, /device:TPU:1, one launch (start us, length us, event | category | flops | bytes accessed | tf_op | source)
XLA Modules:
  0.0 119.8 jit_solution(11090895609242776855)
XLA Ops:
  0.7 0.6 broadcast_in_dim.82
  1.4 15.0 %all-to-all-start = ((s32[64,1,1]{2,1,0:T(1,128)}), s32[64,1,1]{2,1,0:T(1,128)S(1)}, u32[]{:S(2)}, u32[]{:S(2)}) async-start(s32[64,1,1]{2,1,0:T(1,128)} %broadcast_in_dim.82), calls=%async_computation | async-start | bytes 65536 | tf_op jit(solution)/shard_map/all_to_all | solution.py:14
  16.4 0.6 copy-done.4
  17.1 0.5 broadcast.77
  17.6 1.0 reduce.14
  18.6 0.6 reshape.189
  19.3 6.4 %all-to-all-done = s32[64,1,1]{2,1,0:T(1,128)S(1)} async-done(((s32[64,1,1]{2,1,0:T(1,128)}), s32[64,1,1]{2,1,0:T(1,128)S(1)}, u32[]{:S(2)}, u32[]{:S(2)}) %all-to-all-start) | async-done | bytes 288 | tf_op jit(solution)/shard_map/all_to_all | solution.py:14
  25.7 4.8 %all-to-all-start.1 = ((bf16[64,2,256]{2,1,0:T(2,128)(2,1)}), bf16[64,2,256]{2,1,0:T(2,128)(2,1)S(1)}, u32[]{:S(2)}, u32[]{:S(2)}) async-start(bf16[64,2,256]{2,1,0:T(2,128)(2,1)} %reshape.189), calls=%async_computation.1 | async-start | bytes 131072 | tf_op jit(solution)/shard_map/all_to_all | solution.py:14
  30.6 1.2 %reduce.6 = s32[64]{0:T(128)S(1)} reduce(s32[64,1,1]{2,1,0:T(1,128)S(1)} %all-to-all-done, s32[]{:T(128)} %constant.6.clone.1), dimensions={1,2}, to_apply=%all_to_all.29.reduce_sub_computation | reduce | bytes 516 | tf_op jit(solution)/shard_map/all_to_all | solution.py:14
  31.9 8.8 %all-to-all-done.1 = bf16[64,2,256]{2,1,0:T(2,128)(2,1)S(1)} async-done(((bf16[64,2,256]{2,1,0:T(2,128)(2,1)}), bf16[64,2,256]{2,1,0:T(2,128)(2,1)S(1)}, u32[]{:S(2)}, u32[]{:S(2)}) %all-to-all-start.1) | async-done | bytes 65568 | tf_op jit(solution)/shard_map/all_to_all | solution.py:14
  40.7 0.2 convolution_convert_fusion
  41.0 0.7 fusion.21
  41.9 0.8 reshape.191
  42.7 4.4 %all-to-all-start.2 = ((f32[64,1,256]{2,1,0:T(1,128)}), f32[64,1,256]{2,1,0:T(1,128)S(1)}, u32[]{:S(2)}, u32[]{:S(2)}) async-start(f32[64,1,256]{2,1,0:T(1,128)} %reshape.191), calls=%async_computation.2 | async-start | bytes 131072 | tf_op jit(solution)/shard_map/all_to_all | solution.py:14
  47.1 0.4 fusion.11
  47.6 0.2 fusion.9
  48.0 9.3 %all-to-all-done.2 = f32[64,1,256]{2,1,0:T(1,128)S(1)} async-done(((f32[64,1,256]{2,1,0:T(1,128)}), f32[64,1,256]{2,1,0:T(1,128)S(1)}, u32[]{:S(2)}, u32[]{:S(2)}) %all-to-all-start.2) | async-done | bytes 65568 | tf_op jit(solution)/shard_map/all_to_all | solution.py:14
  57.2 0.6 broadcast.78
  57.8 0.8 reduce.15
  58.9 0.5 fusion.1
  59.5 0.2 copy.28
  59.7 15.4 %all_to_all.44 = f32[64,1,516]{2,1,0:T(1,128)S(1)} all-to-all(f32[64,1,516]{2,1,0:T(1,128)S(1)} %copy.28), channel_id=1, replica_groups=mesh['inst'=64,'tp'=8] {'inst'}, dimensions={0} | all-to-all | bytes 264192 | tf_op jit(solution)/shard_map/all_to_all | solution.py:40
  75.1 0.1 reduce_sum.40
  75.4 1.0 reduce.16
  76.5 14.0 %all_to_all.45 = bf16[64,2,256]{2,1,0:T(2,128)(2,1)S(1)} all-to-all(bf16[64,2,256]{2,1,0:T(2,128)(2,1)S(1)} %reshape.193), channel_id=1, replica_groups=mesh['inst'=64,'tp'=8] {'inst'}, dimensions={0} | all-to-all | bytes 131072 | tf_op jit(solution)/shard_map/all_to_all | solution.py:14
  90.5 0.8 copy-done.2
  91.3 0.1 fusion.3
  91.4 13.1 %all_to_all.46 = f32[64,1,64]{2,1,0:T(1,128)S(1)} all-to-all(f32[64,1,64]{2,1,0:T(1,128)S(1)} %bitcast.36), channel_id=1, replica_groups=mesh['inst'=64,'tp'=8] {'inst'}, dimensions={0} | all-to-all | bytes 32768 | tf_op jit(solution)/shard_map/all_to_all | solution.py:107
  104.6 0.5 broadcast.76
  105.1 0.7 reduce.13
  105.9 13.2 %all_to_all.47 = f32[8,1,512]{2,1,0:T(1,128)S(1)} all-to-all(f32[8,1,512]{2,1,0:T(1,128)S(1)} %transpose_reshape.4), channel_id=1, replica_groups=mesh['inst'=64,'tp'=8] {'tp'}, dimensions={0} | all-to-all | bytes 32768 | tf_op jit(solution)/shard_map/all_to_all | solution.py:40
  119.2 0.6 convert_element_type.31
  (37 shorter events, 1.5 us)
Async XLA Ops:
  0.0 41.0 %copy-start = (bf16[32,128,128]{2,1,0:T(8,128)(2,1)S(1)}, bf16[32,128,128]{2,1,0:T(8,128)(2,1)}, u32[]{:S(2)}) copy-start(bf16[32,128,128]{2,1,0:T(8,128)(2,1)} %param.9) | copy-start | bytes 3145732
  1.4 15.0 %copy-start.5 = (s32[32]{0:T(128)S(1)}, s32[32]{0:T(128)}, u32[]{:S(2)}) copy-start(s32[32]{0:T(128)} %param.12) | copy-start | bytes 388
  1.4 24.4 %all-to-all-start = ((s32[64,1,1]{2,1,0:T(1,128)}), s32[64,1,1]{2,1,0:T(1,128)S(1)}, u32[]{:S(2)}, u32[]{:S(2)}) async-start(s32[64,1,1]{2,1,0:T(1,128)} %broadcast_in_dim.82), calls=%async_computation | async-start | bytes 65536 | tf_op jit(solution)/shard_map/all_to_all | solution.py:14
  16.3 0.7 copy-start.4
  25.7 6.1 %copy-start.3 = (s32[32]{0:T(128)S(1)}, s32[32]{0:T(128)}, u32[]{:S(2)}) copy-start(s32[32]{0:T(128)} %param.11) | copy-start | bytes 388
  25.7 15.0 %all-to-all-start.1 = ((bf16[64,2,256]{2,1,0:T(2,128)(2,1)}), bf16[64,2,256]{2,1,0:T(2,128)(2,1)S(1)}, u32[]{:S(2)}, u32[]{:S(2)}) async-start(bf16[64,2,256]{2,1,0:T(2,128)(2,1)} %reshape.189), calls=%async_computation.1 | async-start | bytes 131072 | tf_op jit(solution)/shard_map/all_to_all | solution.py:14
  30.6 16.5 %copy-start.1 = (bf16[32,128,128]{2,1,0:T(8,128)(2,1)S(1)}, bf16[32,128,128]{2,1,0:T(8,128)(2,1)}, u32[]{:S(2)}) copy-start(bf16[32,128,128]{2,1,0:T(8,128)(2,1)} %param.10) | copy-start | bytes 3145732
  42.7 14.6 %all-to-all-start.2 = ((f32[64,1,256]{2,1,0:T(1,128)}), f32[64,1,256]{2,1,0:T(1,128)S(1)}, u32[]{:S(2)}, u32[]{:S(2)}) async-start(f32[64,1,256]{2,1,0:T(1,128)} %reshape.191), calls=%async_computation.2 | async-start | bytes 131072 | tf_op jit(solution)/shard_map/all_to_all | solution.py:14
  90.5 0.8 copy-start.2
where the time goes:
time: 120 us
  blocking collectives  55.8 us (46%)
  waiting for transfers between devices  24.5 us (20%)
  starting transfers between devices  24.2 us (20%)
  local copies, waits for them, and re-layouts  6.63 us (6%)
  other arithmetic  5.72 us (5%)
  matrix products  1.98 us (2%)
    all_to_all x2, blocking collectives, summed_on_arrival(): lax.all_to_all(parts, axis, split_axis=0, concat_axis=0, tiled=True)  28.6 us
    all_to_all x3, waiting for transfers between devices, sent_to_all(): lax.all_to_all(jnp.broadcast_to(x[None], (length, *x.shape)), axis, 0, 0,...  24.5 us
    all_to_all x3, starting transfers between devices, sent_to_all(): lax.all_to_all(jnp.broadcast_to(x[None], (length, *x.shape)), axis, 0, 0,...  24.2 us
    all_to_all x1, blocking collectives, sent_to_all(): lax.all_to_all(jnp.broadcast_to(x[None], (length, *x.shape)), axis, 0, 0,...  14 us
    all_to_all x1, blocking collectives, on_device(): lax.all_to_all(column_part, 'inst', split_axis=0, concat_axis=1, tiled=True)  13.1 us
    unnamed x19, local copies, waits for them, and re-layouts  3.06 us
  transfers between devices with their start and end apart: 3, of which 3 were waited for; matrix products, arithmetic and copies ran while one was open for 4% of the time, Pallas kernels for 0%

commit v1 on v0

v1 whole, which is shorter than its diff:
```python
import functools

import jax
import jax.numpy as jnp
from jax import lax
from jax.experimental import pallas as pl
from jax.experimental.pallas import tpu as pltpu
from jax.sharding import Mesh, PartitionSpec as P

HEAD = 128
NEG_FILL = -1e30
F32, BF16 = jnp.float32, jnp.bfloat16
NT = (((1,), (1,)), ((), ()))
VMEM = pl.BlockSpec(memory_space=pltpu.VMEM)
SMEM = pl.BlockSpec(memory_space=pltpu.SMEM)


def iota(shape, dim):
    return lax.broadcasted_iota(jnp.int32, shape, dim)


def prepare(req_ref, q_ref, w_ref, out_ref):
    feats, cols = w_ref.shape
    eye = (iota((cols, cols), 0) == iota((cols, cols), 1)).astype(F32).astype(BF16)
    turned = lax.dot_general(eye, w_ref[...], NT, preferred_element_type=F32)
    half = cols // 2
    lane = iota((half, HEAD), 1)
    chunks = []
    for m in range(feats // HEAD):
        low = turned[:half, m * HEAD : (m + 1) * HEAD]
        high = turned[half:, m * HEAD : (m + 1) * HEAD]
        chunks.append(jnp.where(lane < 64, low, pltpu.roll(high, 64, 1)).astype(BF16))
        chunks.append(jnp.where(lane < 64, pltpu.roll(low, 64, 1), high).astype(BF16))
    row = iota((8, HEAD), 0)
    tile = jnp.full((8, HEAD), req_ref[0].astype(F32), F32)
    for h in range(4):
        head = q_ref[:, h * HEAD : (h + 1) * HEAD].astype(F32)
        tile = jnp.where(row == h, jnp.broadcast_to(head, (8, HEAD)), tile)
    tile = tile.astype(BF16)
    for d in range(out_ref.shape[0]):
        out_ref[d, 0:half, :] = chunks[d % len(chunks)]
        out_ref[d, half : half + 8, :] = tile


def three_parts(x):
    hi = x.astype(BF16).astype(F32)
    rest = x - hi
    mid = rest.astype(BF16).astype(F32)
    return hi, mid, rest - mid


def attend(owner_ref, fill_ref, got_ref, k_ref, v_ref, out_ref, peak_ref, mix_ref, sum_ref):
    n_slots = got_ref.shape[0]
    n_pages = k_ref.shape[0]
    n_req = peak_ref.shape[0] - 1
    rows = got_ref[:, 32:40, :].astype(F32).reshape(n_slots * 8, HEAD)
    rows_bf = rows.astype(BF16)
    first = (iota((8, HEAD), 1) == 0).astype(F32).astype(BF16)
    ids = lax.dot_general(first, rows_bf, NT, preferred_element_type=F32)
    blocks = [
        pltpu.roll(ids[:, b * HEAD : (b + 1) * HEAD], HEAD - 4, 1) for b in range(n_slots * 8 // HEAD)
    ]
    here = (iota((8, HEAD), 1) % 8 == iota((8, HEAD), 0)) & (iota((8, HEAD), 0) < 4)
    blocks = [jnp.where(here, b, -5.0) for b in blocks]
    owners = [owner_ref[p] for p in range(n_pages)]
    picks = []
    for p in range(n_pages):
        wanted = jnp.where(owners[p] >= 0, owners[p], -7).astype(F32)
        picks.append(jnp.concatenate([jnp.where(b == wanted, 1.0, 0.0) for b in blocks], axis=1))
    pick = jnp.concatenate(picks, axis=0).astype(BF16)
    page_q = jnp.dot(pick, rows_bf, preferred_element_type=F32)

    peak_ref[...] = jnp.full(peak_ref.shape, NEG_FILL, F32)
    mix_ref[...] = jnp.zeros(mix_ref.shape, F32)
    sum_ref[...] = jnp.zeros(sum_ref.shape, F32)
    token = iota((8, HEAD), 1)
    peaks, totals, outs = [], [], []
    for p in range(n_pages):
        score = lax.dot_general(
            page_q[p * 8 : (p + 1) * 8].astype(BF16), k_ref[p], NT, preferred_element_type=F32
        ) * (HEAD**-0.5)
        score = jnp.where(token < fill_ref[p], score, NEG_FILL)
        peak = jnp.max(score, axis=1, keepdims=True)
        e = jnp.exp(score - peak)
        totals.append(jnp.sum(e, axis=1, keepdims=True))
        outs.append(jnp.dot(e.astype(BF16), v_ref[p], preferred_element_type=F32))
        peaks.append(jnp.broadcast_to(peak, (8, HEAD)))
    index = [jnp.where(o >= 0, o, n_req) for o in owners]
    for p in range(n_pages):
        peak_ref[index[p]] = jnp.maximum(peak_ref[index[p]], peaks[p])
    for p in range(n_pages):
        weight = jnp.exp(peaks[p] - peak_ref[index[p]])
        mix_ref[index[p]] += weight * outs[p]
        sum_ref[index[p]] += weight * totals[p]

    n_rows = n_req * 8
    lane = iota((n_rows, HEAD), 1)
    mix = mix_ref[0:n_req].reshape(n_rows, HEAD)
    total = sum_ref[0:n_req].reshape(n_rows, HEAD)
    hi, mid, low = three_parts(peak_ref[0:n_req].reshape(n_rows, HEAD))
    total_hi = total.astype(BF16).astype(F32)
    stats = jnp.where(
        lane < 80,
        hi,
        jnp.where(lane < 96, mid, jnp.where(lane < 112, low, jnp.where(lane < 120, total_hi, total - total_hi))),
    )
    data = jnp.concatenate([mix.astype(BF16), stats.astype(BF16)], axis=1)
    place = (iota((n_slots, n_slots * 8), 1) == iota((n_slots, n_slots * 8), 0) * 8 + 4)
    slot_id = jnp.dot(place.astype(F32).astype(BF16), rows_bf, preferred_element_type=F32)[:, 0:1]
    col = iota((n_slots, n_rows), 1)
    owns = slot_id == (col // 8).astype(F32)
    lane8 = iota((n_slots, HEAD), 1)
    for h in range(4):
        chosen = jnp.where(owns & (col % 8 == h), 1.0, 0.0).astype(BF16)
        picked = jnp.dot(chosen, data, preferred_element_type=F32)
        o, st = picked[:, :HEAD], picked[:, HEAD:]
        left = jnp.where(lane8 < 64, o, st)
        right = jnp.where(lane8 < 64, pltpu.roll(o, 64, 1), st)
        for z in range(n_slots // 8):
            out_ref[z * 8 + 2 * h] = left[z * 8 : (z + 1) * 8].astype(BF16)
            out_ref[z * 8 + 2 * h + 1] = right[z * 8 : (z + 1) * 8].astype(BF16)


def project(part_ref, got_ref, out_ref):
    n_src = part_ref.shape[0]
    flat = part_ref[...].astype(F32).reshape(n_src * 8, HEAD)
    src = iota((HEAD, 2 * HEAD), 0)
    dst = iota((HEAD, 2 * HEAD), 1)
    is_peak = (src == 64) | (src == 80) | (src == 96)
    is_total = (src == 112) | (src == 120)
    spread = jnp.where(((dst < HEAD) & is_peak) | ((dst >= HEAD) & is_total), 1.0, 0.0).astype(BF16)
    stats = jnp.dot(flat.astype(BF16), spread, preferred_element_type=F32)
    total = stats[:, HEAD:].reshape(n_src, 8, HEAD)
    peak = jnp.where(total > 0.0, stats[:, :HEAD].reshape(n_src, 8, HEAD), NEG_FILL)
    top = jnp.max(peak, axis=0)
    factor = jnp.exp(peak - top[None])
    whole = jnp.sum(factor * total, axis=0)
    mix = jnp.sum(factor * flat.reshape(n_src, 8, HEAD), axis=0)
    attention = mix / jnp.where(whole > 0.0, whole, 1.0)
    attention = jnp.where(iota((8, HEAD), 1) < 64, attention, 0.0)
    both = jnp.concatenate([attention, pltpu.roll(attention, 64, 1)], axis=0).astype(BF16)
    weights = got_ref[:, 0:32, :].reshape(n_src * 32, HEAD)
    result = lax.dot_general(both, weights, NT, preferred_element_type=F32)
    for y in range(out_ref.shape[1]):
        for h in range(2):
            for half in range(2):
                at = (y * 2 + half) * HEAD
                out_ref[:, y, h * 2 + half, :] = result[h * 8 : (h + 1) * 8, at : at + HEAD]


def finish(part_ref, out_ref):
    v = jnp.sum(part_ref[...], axis=0)
    lane = iota((1, HEAD), 1)
    for q in range(4):
        a = v[q // 2 : q // 2 + 1]
        b = v[2 + q // 2 : 3 + q // 2]
        shifts = (0, 32, 32, 64) if q % 2 == 0 else (64, 96, 96, 0)
        moved = [
            x if s == 0 else pltpu.roll(x, s, 1) for x, s in zip((a, b, a, b), shifts)
        ]
        block = jnp.where(
            lane < 32, moved[0], jnp.where(lane < 64, moved[1], jnp.where(lane < 96, moved[2], moved[3]))
        )
        out_ref[:, q * HEAD : (q + 1) * HEAD] = block.astype(BF16)


def on_device(queries, slot_request, key_pages, value_pages, page_owner, page_fill, out_weight, axes):
    z, w, y = axes
    nz, nw, ny = (lax.axis_size(a) for a in axes)
    n_inst = nz * nw
    n_req = 32
    sent = pl.pallas_call(
        prepare,
        out_shape=jax.ShapeDtypeStruct((n_inst, 40, HEAD), BF16),
        in_specs=[SMEM, VMEM, VMEM],
        out_specs=VMEM,
        name="prepare",
    )(slot_request, queries, out_weight)
    got = lax.all_to_all(sent, (z, w), 0, 0, tiled=True)
    parts = pl.pallas_call(
        attend,
        out_shape=jax.ShapeDtypeStruct((n_inst, 8, HEAD), BF16),
        in_specs=[SMEM, SMEM, VMEM, VMEM, VMEM],
        out_specs=VMEM,
        scratch_shapes=[pltpu.VMEM((n_req + 1, 8, HEAD), F32)] * 3,
        name="attend",
    )(page_owner, page_fill, got, key_pages, value_pages)
    parts = lax.all_to_all(parts, (z, w), 0, 0, tiled=True)
    columns = pl.pallas_call(
        project,
        out_shape=jax.ShapeDtypeStruct((nw, ny, 4, HEAD), F32),
        in_specs=[VMEM, VMEM],
        out_specs=VMEM,
        name="project",
    )(parts, got)
    columns = lax.all_to_all(columns.reshape(nw * ny, 4, HEAD), (w, y), 0, 0, tiled=True)
    return pl.pallas_call(
        finish,
        out_shape=jax.ShapeDtypeStruct((1, 4 * HEAD), BF16),
        in_specs=[VMEM],
        out_specs=VMEM,
        name="finish",
    )(columns)


def solution(mesh):
    axes = ("z", "w", "y")
    inst, tp = mesh.devices.shape
    cut = Mesh(mesh.devices.reshape(inst // 8, 8, tp), axes)
    i = axes[:2]
    return jax.shard_map(
        functools.partial(on_device, axes=axes),
        mesh=cut,
        in_specs=(P(i, "y"), P(i), P(i, None, "y"), P(i, None, "y"), P(i), P(i), P("y", i)),
        out_specs=P(i, "y"),
        check_vma=False,
    )
```

time: 120 us -> 90.6 us (0.76)
  waiting for transfers between devices: 24.5 us -> 0 us
  starting transfers between devices: 24.2 us -> 0 us
  Pallas kernels: 0 us -> 16.7 us
  blocking collectives: 55.8 us -> 71.3 us
  other arithmetic: 5.72 us -> 0 us
  local copies, waits for them, and re-layouts: 6.63 us -> 1.58 us
  matrix products: 1.98 us -> 0 us
    all_to_all x3 -> x0, waiting for transfers between devices: 24.5 us -> none  [sent_to_all(): lax.all_to_all(jnp.broadcast_to(x[None], (length, *x.shape)), axis, 0, 0,...]
    all_to_all x3 -> x0, starting transfers between devices: 24.2 us -> none  [sent_to_all(): lax.all_to_all(jnp.broadcast_to(x[None], (length, *x.shape)), axis, 0, 0,...]
    pallas_call x0 -> x4, Pallas kernels: none -> 16.7 us  [the longest x1 10.4 us: on_device(): pl.pallas_call(attend, out_shape=jax.ShapeDtypeStruct((n_inst, 8, HEAD),...]
    all_to_all x4 -> x3, blocking collectives: 55.8 us -> 71.3 us  [the longest x1 35.3 us: on_device(): got = lax.all_to_all(sent, (z, w), 0, 0, tiled=True)]
    all_to_all x3 -> x0, other arithmetic: 2.79 us -> none  [the longest x2 2.06 us: sent_to_all(): lax.all_to_all(jnp.broadcast_to(x[None], (length, *x.shape)), axis, 0, 0,...]
    broadcast_in_dim x2 -> x0, other arithmetic: 2.02 us -> none  [sent_to_all(): jnp.broadcast_to(x[None], (length, *x.shape))]
    dot_general x5 -> x0, matrix products: 1.98 us -> none  [the longest x1 0.72 us: on_device(): jnp.einsum('pkgd,ptkd->pkgt', query_portion, key_portion, preferred_eleme...]
    unnamed x19 -> x1, local copies, waits for them, and re-layouts: 3.06 us -> 1.58 us
  transfers between devices with their start and end apart: 3 -> 0, of which waited for: 3 -> 0; matrix products, arithmetic and copies ran while one was open for 4% -> 0% of each run, Pallas kernels for 0% -> 0%
where the time goes in v1:
time: 90.6 us; the launch traced here: 90.2 us
  blocking collectives  71.3 us (79%)
  Pallas kernels  16.7 us (18%)
  local copies, waits for them, and re-layouts  1.58 us (2%)
    all_to_all x1, blocking collectives, on_device(): got = lax.all_to_all(sent, (z, w), 0, 0, tiled=True)  35.3 us
    all_to_all x1, blocking collectives, on_device(): lax.all_to_all(columns.reshape(nw * ny, 4, HEAD), (w, y), 0, 0, tiled=True)  19 us
    all_to_all x1, blocking collectives, on_device(): parts = lax.all_to_all(parts, (z, w), 0, 0, tiled=True)  17 us
    pallas_call x1, Pallas kernels, on_device(): pl.pallas_call(attend, out_shape=jax.ShapeDtypeStruct((n_inst, 8, HEAD),...  10.4 us
    pallas_call x1, Pallas kernels, on_device(): pl.pallas_call(project, out_shape=jax.ShapeDtypeStruct((nw, ny, 4, HEAD),...  2.57 us
    pallas_call x1, Pallas kernels, on_device(): pl.pallas_call(prepare, out_shape=jax.ShapeDtypeStruct((n_inst, 40, HEAD)...  2.04 us

profile of v1, /device:TPU:1, one launch (start us, length us, event | category | flops | bytes accessed | tf_op | source)
XLA Modules:
  0.0 90.2 jit_solution(9324127932559122055)
XLA Ops:
  0.7 1.6 %copy.8.w_ref = bf16[512,64]{1,0:T(8,128)(2,1)} copy(bf16[512,64]{0,1:T(8,128)(2,1)} %param.13) | data formatting | bytes 131072 | tf_op args[6]
  2.2 2.0 %prepare.1 = bf16[64,40,128]{2,1,0:T(8,128)(2,1)} custom-call(s32[1]{0:T(128)S(6)} %copy.9.req_ref, bf16[1,512]{1,0:T(2,128)(2,1)} %q_ref.1, bf16[512,64]{1,0:T(8,128)(2,1)} %copy.8.w_ref), custom_call_target="tpu_custom_call" | custom-call | tf_op jit(solution)/shard_map/prepare/pallas_call | solution.py:172
  4.3 35.3 %all_to_all.15.got_ref = bf16[64,40,128]{2,1,0:T(8,128)(2,1)} all-to-all(bf16[64,40,128]{2,1,0:T(8,128)(2,1)} %prepare.1), channel_id=1, replica_groups=mesh['z'=8,'w'=8,'y'=8] {'z','w'}, dimensions={0} | all-to-all | bytes 1310720 | tf_op jit(solution)/shard_map/all_to_all | solution.py:179
  39.6 10.4 %attend.1 = bf16[64,8,128]{2,1,0:T(8,128)(2,1)} custom-call(s32[32]{0:T(128)} %owner_ref.1, s32[32]{0:T(128)} %fill_ref.1, bf16[64,40,128]{2,1,0:T(8,128)(2,1)} %all_to_all.15.got_ref, bf16[32,128,128]{2,1,0:T(8,128)(2,1)} %k_ref.1, bf16[32,128,128]{2,1,0:T(8,128)(2,1)} %v_ref.1), custom_call_target="tpu_custom_call" | custom-call | tf_op jit(solution)/shard_map/attend/pallas_call | solution.py:180
  50.0 17.0 %all_to_all.16.part_ref = bf16[64,8,128]{2,1,0:T(8,128)(2,1)} all-to-all(bf16[64,8,128]{2,1,0:T(8,128)(2,1)} %attend.1), channel_id=1, replica_groups=mesh['z'=8,'w'=8,'y'=8] {'z','w'}, dimensions={0} | all-to-all | bytes 262144 | tf_op jit(solution)/shard_map/all_to_all | solution.py:188
  67.0 2.6 %project.1 = f32[8,8,4,128]{3,2,1,0:T(4,128)} custom-call(bf16[64,8,128]{2,1,0:T(8,128)(2,1)} %all_to_all.16.part_ref, bf16[64,40,128]{2,1,0:T(8,128)(2,1)} %all_to_all.15.got_ref), custom_call_target="tpu_custom_call" | custom-call | tf_op jit(solution)/shard_map/project/pallas_call | solution.py:189
  69.5 19.0 %all_to_all.17.part_ref = f32[64,4,128]{2,1,0:T(4,128)} all-to-all(f32[64,4,128]{2,1,0:T(4,128)} %bitcast.1), channel_id=1, replica_groups=mesh['z'=8,'w'=8,'y'=8] {'w','y'}, dimensions={0} | all-to-all | bytes 262144 | tf_op jit(solution)/shard_map/all_to_all | solution.py:196
  88.6 1.6 %finish.1 = bf16[1,512]{1,0:T(2,128)(2,1)} custom-call(f32[64,4,128]{2,1,0:T(4,128)} %all_to_all.17.part_ref), custom_call_target="tpu_custom_call" | custom-call | tf_op jit(solution)/shard_map/finish/pallas_call | solution.py:197

commit v2 on v1

--- a/solution.py
+++ b/solution.py
@@ -20,15 +20,13 @@
 
 
 def prepare(req_ref, q_ref, w_ref, out_ref):
-    feats, cols = w_ref.shape
-    eye = (iota((cols, cols), 0) == iota((cols, cols), 1)).astype(F32).astype(BF16)
-    turned = lax.dot_general(eye, w_ref[...], NT, preferred_element_type=F32)
+    cols, feats = w_ref.shape
     half = cols // 2
     lane = iota((half, HEAD), 1)
     chunks = []
     for m in range(feats // HEAD):
-        low = turned[:half, m * HEAD : (m + 1) * HEAD]
-        high = turned[half:, m * HEAD : (m + 1) * HEAD]
+        low = w_ref[:half, m * HEAD : (m + 1) * HEAD].astype(F32)
+        high = w_ref[half:, m * HEAD : (m + 1) * HEAD].astype(F32)
         chunks.append(jnp.where(lane < 64, low, pltpu.roll(high, 64, 1)).astype(BF16))
         chunks.append(jnp.where(lane < 64, pltpu.roll(low, 64, 1), high).astype(BF16))
     row = iota((8, HEAD), 0)
@@ -169,13 +167,15 @@
     nz, nw, ny = (lax.axis_size(a) for a in axes)
     n_inst = nz * nw
     n_req = 32
+    limit = pltpu.CompilerParams(vmem_limit_bytes=12 << 20)
     sent = pl.pallas_call(
         prepare,
         out_shape=jax.ShapeDtypeStruct((n_inst, 40, HEAD), BF16),
         in_specs=[SMEM, VMEM, VMEM],
         out_specs=VMEM,
+        compiler_params=limit,
         name="prepare",
-    )(slot_request, queries, out_weight)
+    )(slot_request, queries, out_weight.T)
     got = lax.all_to_all(sent, (z, w), 0, 0, tiled=True)
     parts = pl.pallas_call(
         attend,
@@ -183,6 +183,7 @@
         in_specs=[SMEM, SMEM, VMEM, VMEM, VMEM],
         out_specs=VMEM,
         scratch_shapes=[pltpu.VMEM((n_req + 1, 8, HEAD), F32)] * 3,
+        compiler_params=limit,
         name="attend",
     )(page_owner, page_fill, got, key_pages, value_pages)
     parts = lax.all_to_all(parts, (z, w), 0, 0, tiled=True)
@@ -191,6 +192,7 @@
         out_shape=jax.ShapeDtypeStruct((nw, ny, 4, HEAD), F32),
         in_specs=[VMEM, VMEM],
         out_specs=VMEM,
+        compiler_params=limit,
         name="project",
     )(parts, got)
     columns = lax.all_to_all(columns.reshape(nw * ny, 4, HEAD), (w, y), 0, 0, tiled=True)
@@ -199,6 +201,7 @@
         out_shape=jax.ShapeDtypeStruct((1, 4 * HEAD), BF16),
         in_specs=[VMEM],
         out_specs=VMEM,
+        compiler_params=limit,
         name="finish",
     )(columns)
 

time: 90.6 us -> 84.4 us (0.932)
  Pallas kernels: 16.7 us -> 10.2 us
  local copies, waits for them, and re-layouts: 1.58 us -> 2.75 us
    pallas_call x1, Pallas kernels: 2.04 us -> 0.11 us  [on_device(): pl.pallas_call(prepare, out_shape=jax.ShapeDtypeStruct((n_inst, 40, HEAD)...]
    pallas_call x1, Pallas kernels: 10.4 us -> 8.57 us  [on_device(): pl.pallas_call(attend, out_shape=jax.ShapeDtypeStruct((n_inst, 8, HEAD),...]
    pallas_call x1, Pallas kernels: 2.57 us -> 0.75 us  [on_device(): pl.pallas_call(project, out_shape=jax.ShapeDtypeStruct((nw, ny, 4, HEAD),...]
    unnamed x1 -> x12, local copies, waits for them, and re-layouts: 1.58 us -> 2.75 us
where the time goes in v2:
time: 84.4 us; the launch traced here: 84.1 us
  blocking collectives  70.4 us (83%)
  Pallas kernels  10.2 us (12%)
  local copies, waits for them, and re-layouts  2.75 us (3%)
    all_to_all x1, blocking collectives, on_device(): got = lax.all_to_all(sent, (z, w), 0, 0, tiled=True)  35 us
    all_to_all x1, blocking collectives, on_device(): lax.all_to_all(columns.reshape(nw * ny, 4, HEAD), (w, y), 0, 0, tiled=True)  18.7 us
    all_to_all x1, blocking collectives, on_device(): parts = lax.all_to_all(parts, (z, w), 0, 0, tiled=True)  16.7 us
    pallas_call x1, Pallas kernels, on_device(): pl.pallas_call(attend, out_shape=jax.ShapeDtypeStruct((n_inst, 8, HEAD),...  8.57 us
    unnamed x12, local copies, waits for them, and re-layouts  2.75 us

profile of v2, /device:TPU:1, one launch (start us, length us, event | category | flops | bytes accessed | tf_op | source)
XLA Modules:
  0.0 84.1 jit_solution(2148092917137607831)
XLA Ops:
  0.0 0.0 copy-start
  0.7 0.0 copy-start.2
  0.8 0.8 copy-done.2
  1.6 0.0 copy-start.3
  1.6 0.7 copy-done.3
  2.3 0.1 prepare.1
  2.4 0.0 copy-start.4
  2.4 0.0 copy-start.5
  2.4 35.0 %all_to_all.15.got_ref = bf16[64,40,128]{2,1,0:T(8,128)(2,1)S(1)} all-to-all(bf16[64,40,128]{2,1,0:T(8,128)(2,1)S(1)} %prepare.1), channel_id=1, replica_groups=mesh['z'=8,'w'=8,'y'=8] {'z','w'}, dimensions={0} | all-to-all | bytes 1310720 | tf_op jit(solution)/shard_map/all_to_all | solution.py:179
  37.4 0.0 copy-done
  37.4 0.0 copy-done.4
  37.4 0.0 copy-done.5
  37.4 0.0 copy-start.1
  37.4 1.2 %copy-done.1 = bf16[32,128,128]{2,1,0:T(8,128)(2,1)S(1)} copy-done((bf16[32,128,128]{2,1,0:T(8,128)(2,1)S(1)}, bf16[32,128,128]{2,1,0:T(8,128)(2,1)}, u32[]{:S(2)}) %copy-start.1) | copy-done | bytes 1048600
  38.6 8.6 %attend.1 = bf16[64,8,128]{2,1,0:T(8,128)(2,1)S(1)} custom-call(s32[32]{0:T(128)S(1)} %copy-done.4, s32[32]{0:T(128)S(1)} %copy-done.5, bf16[64,40,128]{2,1,0:T(8,128)(2,1)S(1)} %all_to_all.15.got_ref, bf16[32,128,128]{2,1,0:T(8,128)(2,1)S(1)} %copy-done, bf16[32,128,128]{2,1,0:T(8,128)(2,1)S(1)} %copy-done.1), custom_call_target="tpu_custom_call" | custom-call | tf_op jit(solution)/shard_map/attend/pallas_call | solution.py:180
  47.2 16.7 %all_to_all.16.part_ref = bf16[64,8,128]{2,1,0:T(8,128)(2,1)S(1)} all-to-all(bf16[64,8,128]{2,1,0:T(8,128)(2,1)S(1)} %attend.1), channel_id=1, replica_groups=mesh['z'=8,'w'=8,'y'=8] {'z','w'}, dimensions={0} | all-to-all | bytes 262144 | tf_op jit(solution)/shard_map/all_to_all | solution.py:189
  63.9 0.8 project.1
  64.6 18.7 %all_to_all.17.part_ref = f32[64,4,128]{2,1,0:T(4,128)S(1)} all-to-all(f32[64,4,128]{2,1,0:T(4,128)S(1)} %bitcast.2), channel_id=1, replica_groups=mesh['z'=8,'w'=8,'y'=8] {'w','y'}, dimensions={0} | all-to-all | bytes 262144 | tf_op jit(solution)/shard_map/all_to_all | solution.py:198
  83.4 0.7 finish.1
Async XLA Ops:
  0.0 37.4 %copy-start = (bf16[32,128,128]{2,1,0:T(8,128)(2,1)S(1)}, bf16[32,128,128]{2,1,0:T(8,128)(2,1)}, u32[]{:S(2)}) copy-start(bf16[32,128,128]{2,1,0:T(8,128)(2,1)} %k_ref.1) | copy-start | bytes 3145732
  0.7 0.8 copy-start.2
  1.6 0.7 copy-start.3
  2.4 35.0 %copy-start.4 = (s32[32]{0:T(128)S(1)}, s32[32]{0:T(128)}, u32[]{:S(2)}) copy-start(s32[32]{0:T(128)} %owner_ref.1) | copy-start | bytes 388
  2.4 35.0 %copy-start.5 = (s32[32]{0:T(128)S(1)}, s32[32]{0:T(128)}, u32[]{:S(2)}) copy-start(s32[32]{0:T(128)} %fill_ref.1) | copy-start | bytes 388
  37.4 1.2 %copy-start.1 = (bf16[32,128,128]{2,1,0:T(8,128)(2,1)S(1)}, bf16[32,128,128]{2,1,0:T(8,128)(2,1)}, u32[]{:S(2)}) copy-start(bf16[32,128,128]{2,1,0:T(8,128)(2,1)} %v_ref.1) | copy-start | bytes 3145732

commit v3 on v2

--- a/solution.py
+++ b/solution.py
@@ -13,13 +13,20 @@
 NT = (((1,), (1,)), ((), ()))
 VMEM = pl.BlockSpec(memory_space=pltpu.VMEM)
 SMEM = pl.BlockSpec(memory_space=pltpu.SMEM)
+HBM = pl.BlockSpec(memory_space=pltpu.HBM)
 
 
 def iota(shape, dim):
     return lax.broadcasted_iota(jnp.int32, shape, dim)
 
 
-def prepare(req_ref, q_ref, w_ref, out_ref):
+def prepare(req_ref, q_hbm, w_hbm, v_hbm, out_ref, v_ref, q_ref, w_ref, sems):
+    pairs = ((q_hbm, q_ref), (w_hbm, w_ref), (v_hbm, v_ref))
+    copies = [pltpu.make_async_copy(a, b, sems.at[n]) for n, (a, b) in enumerate(pairs)]
+    for copy in copies:
+        copy.start()
+    for copy in copies[:2]:
+        copy.wait()
     cols, feats = w_ref.shape
     half = cols // 2
     lane = iota((half, HEAD), 1)
@@ -38,6 +45,11 @@
     for d in range(out_ref.shape[0]):
         out_ref[d, 0:half, :] = chunks[d % len(chunks)]
         out_ref[d, half : half + 8, :] = tile
+    copies[2].wait()
+
+
+def keep(x):
+    return pltpu.with_memory_space_constraint(x, pltpu.HBM)
 
 
 def three_parts(x):
@@ -50,70 +62,82 @@
 def attend(owner_ref, fill_ref, got_ref, k_ref, v_ref, out_ref, peak_ref, mix_ref, sum_ref):
     n_slots = got_ref.shape[0]
     n_pages = k_ref.shape[0]
+    n_pairs = n_pages // 2
     n_req = peak_ref.shape[0] - 1
-    rows = got_ref[:, 32:40, :].astype(F32).reshape(n_slots * 8, HEAD)
-    rows_bf = rows.astype(BF16)
-    first = (iota((8, HEAD), 1) == 0).astype(F32).astype(BF16)
-    ids = lax.dot_general(first, rows_bf, NT, preferred_element_type=F32)
+    row8 = iota((8, HEAD), 0)
+    lane = iota((8, HEAD), 1)
+    first = row8 < 4
+    rows_bf = got_ref[:, 32:40, :].astype(F32).reshape(n_slots * 8, HEAD).astype(BF16)
+    unit = (lane == 0).astype(F32).astype(BF16)
+    ids = lax.dot_general(unit, rows_bf, NT, preferred_element_type=F32)
+    here = (lane % 8) == (row8 % 4)
     blocks = [
-        pltpu.roll(ids[:, b * HEAD : (b + 1) * HEAD], HEAD - 4, 1) for b in range(n_slots * 8 // HEAD)
+        jnp.where(here, pltpu.roll(ids[:, b * HEAD : (b + 1) * HEAD], HEAD - 4, 1), -5.0)
+        for b in range(n_slots * 8 // HEAD)
     ]
-    here = (iota((8, HEAD), 1) % 8 == iota((8, HEAD), 0)) & (iota((8, HEAD), 0) < 4)
-    blocks = [jnp.where(here, b, -5.0) for b in blocks]
     owners = [owner_ref[p] for p in range(n_pages)]
     picks = []
-    for p in range(n_pages):
-        wanted = jnp.where(owners[p] >= 0, owners[p], -7).astype(F32)
-        picks.append(jnp.concatenate([jnp.where(b == wanted, 1.0, 0.0) for b in blocks], axis=1))
+    for i in range(n_pairs):
+        a, b = owners[2 * i], owners[2 * i + 1]
+        wanted = jnp.where(first, jnp.where(a >= 0, a, -7), jnp.where(b >= 0, b, -7)).astype(F32)
+        picks.append(jnp.concatenate([jnp.where(x == wanted, 1.0, 0.0) for x in blocks], axis=1))
     pick = jnp.concatenate(picks, axis=0).astype(BF16)
     page_q = jnp.dot(pick, rows_bf, preferred_element_type=F32)
-
+    scores = []
+    for i in range(n_pairs):
+        pair = k_ref[2 * i : 2 * i + 2].reshape(2 * HEAD, HEAD)
+        s = lax.dot_general(page_q[8 * i : 8 * i + 8].astype(BF16), pair, NT, preferred_element_type=F32)
+        s = jnp.where(first, s[:, :HEAD], s[:, HEAD:])
+        fill = jnp.where(first, fill_ref[2 * i], fill_ref[2 * i + 1])
+        scores.append(jnp.where(lane < fill, s * (HEAD**-0.5), NEG_FILL))
+    score = jnp.concatenate(scores, axis=0)
+    peak = jnp.broadcast_to(jnp.max(score, axis=1, keepdims=True), score.shape)
+    e = jnp.exp(score - peak)
+    total = jnp.broadcast_to(jnp.sum(e, axis=1, keepdims=True), score.shape)
+    low = (iota(e.shape, 0) % 8) < 4
+    spread = jnp.concatenate([jnp.where(low, e, 0.0), jnp.where(low, 0.0, e)], axis=1)
+    outs = []
+    for i in range(n_pairs):
+        pair = v_ref[2 * i : 2 * i + 2].reshape(2 * HEAD, HEAD)
+        outs.append(jnp.dot(spread[8 * i : 8 * i + 8].astype(BF16), pair, preferred_element_type=F32))
     peak_ref[...] = jnp.full(peak_ref.shape, NEG_FILL, F32)
     mix_ref[...] = jnp.zeros(mix_ref.shape, F32)
     sum_ref[...] = jnp.zeros(sum_ref.shape, F32)
-    token = iota((8, HEAD), 1)
-    peaks, totals, outs = [], [], []
-    for p in range(n_pages):
-        score = lax.dot_general(
-            page_q[p * 8 : (p + 1) * 8].astype(BF16), k_ref[p], NT, preferred_element_type=F32
-        ) * (HEAD**-0.5)
-        score = jnp.where(token < fill_ref[p], score, NEG_FILL)
-        peak = jnp.max(score, axis=1, keepdims=True)
-        e = jnp.exp(score - peak)
-        totals.append(jnp.sum(e, axis=1, keepdims=True))
-        outs.append(jnp.dot(e.astype(BF16), v_ref[p], preferred_element_type=F32))
-        peaks.append(jnp.broadcast_to(peak, (8, HEAD)))
     index = [jnp.where(o >= 0, o, n_req) for o in owners]
     for p in range(n_pages):
-        peak_ref[index[p]] = jnp.maximum(peak_ref[index[p]], peaks[p])
+        mine = first if p % 2 == 0 else jnp.logical_not(first)
+        at = 8 * (p // 2)
+        peak_ref[index[p]] = jnp.maximum(peak_ref[index[p]], jnp.where(mine, peak[at : at + 8], NEG_FILL))
+    every = peak_ref[...]
+    peak_ref[...] = jnp.maximum(every, pltpu.roll(every, 4, 1))
     for p in range(n_pages):
-        weight = jnp.exp(peaks[p] - peak_ref[index[p]])
-        mix_ref[index[p]] += weight * outs[p]
-        sum_ref[index[p]] += weight * totals[p]
-
+        mine = first if p % 2 == 0 else jnp.logical_not(first)
+        at = 8 * (p // 2)
+        weight = jnp.where(mine, jnp.exp(peak[at : at + 8] - peak_ref[index[p]]), 0.0)
+        mix_ref[index[p]] += weight * outs[p // 2]
+        sum_ref[index[p]] += weight * total[at : at + 8]
     n_rows = n_req * 8
-    lane = iota((n_rows, HEAD), 1)
-    mix = mix_ref[0:n_req].reshape(n_rows, HEAD)
-    total = sum_ref[0:n_req].reshape(n_rows, HEAD)
-    hi, mid, low = three_parts(peak_ref[0:n_req].reshape(n_rows, HEAD))
+    mix = mix_ref[0:n_req]
+    mix = (mix + pltpu.roll(mix, 4, 1)).reshape(n_rows, HEAD)
+    total = sum_ref[0:n_req]
+    total = (total + pltpu.roll(total, 4, 1)).reshape(n_rows, HEAD)
+    lane_n = iota((n_rows, HEAD), 1)
+    hi, mid, rest = three_parts(peak_ref[0:n_req].reshape(n_rows, HEAD))
     total_hi = total.astype(BF16).astype(F32)
-    stats = jnp.where(
-        lane < 80,
-        hi,
-        jnp.where(lane < 96, mid, jnp.where(lane < 112, low, jnp.where(lane < 120, total_hi, total - total_hi))),
-    )
+    stats = jnp.where(lane_n < 80, hi, jnp.where(lane_n < 96, mid, jnp.where(lane_n < 112, rest, jnp.where(lane_n < 120, total_hi, total - total_hi))))
     data = jnp.concatenate([mix.astype(BF16), stats.astype(BF16)], axis=1)
-    place = (iota((n_slots, n_slots * 8), 1) == iota((n_slots, n_slots * 8), 0) * 8 + 4)
-    slot_id = jnp.dot(place.astype(F32).astype(BF16), rows_bf, preferred_element_type=F32)[:, 0:1]
+    place = iota((n_slots, n_slots * 8), 1) == iota((n_slots, n_slots * 8), 0) * 8 + 4
+    slot_id = jnp.dot(place.astype(F32).astype(BF16), rows_bf, preferred_element_type=F32)
+    slot_id = jnp.concatenate([slot_id, slot_id], axis=1)
     col = iota((n_slots, n_rows), 1)
     owns = slot_id == (col // 8).astype(F32)
-    lane8 = iota((n_slots, HEAD), 1)
+    left64 = iota((n_slots, HEAD), 1) < 64
     for h in range(4):
         chosen = jnp.where(owns & (col % 8 == h), 1.0, 0.0).astype(BF16)
         picked = jnp.dot(chosen, data, preferred_element_type=F32)
         o, st = picked[:, :HEAD], picked[:, HEAD:]
-        left = jnp.where(lane8 < 64, o, st)
-        right = jnp.where(lane8 < 64, pltpu.roll(o, 64, 1), st)
+        left = jnp.where(left64, o, st)
+        right = jnp.where(left64, pltpu.roll(o, 64, 1), st)
         for z in range(n_slots // 8):
             out_ref[z * 8 + 2 * h] = left[z * 8 : (z + 1) * 8].astype(BF16)
             out_ref[z * 8 + 2 * h + 1] = right[z * 8 : (z + 1) * 8].astype(BF16)
@@ -168,14 +192,19 @@
     n_inst = nz * nw
     n_req = 32
     limit = pltpu.CompilerParams(vmem_limit_bytes=12 << 20)
-    sent = pl.pallas_call(
+    sent, values = pl.pallas_call(
         prepare,
-        out_shape=jax.ShapeDtypeStruct((n_inst, 40, HEAD), BF16),
-        in_specs=[SMEM, VMEM, VMEM],
-        out_specs=VMEM,
+        out_shape=[jax.ShapeDtypeStruct((n_inst, 40, HEAD), BF16), jax.ShapeDtypeStruct(value_pages.shape, BF16)],
+        in_specs=[SMEM, HBM, HBM, HBM],
+        out_specs=[VMEM, VMEM],
+        scratch_shapes=[
+            pltpu.VMEM(queries.shape, BF16),
+            pltpu.VMEM(out_weight.shape[::-1], BF16),
+            pltpu.SemaphoreType.DMA((3,)),
+        ],
         compiler_params=limit,
         name="prepare",
-    )(slot_request, queries, out_weight.T)
+    )(slot_request, keep(queries), keep(out_weight.T), keep(value_pages))
     got = lax.all_to_all(sent, (z, w), 0, 0, tiled=True)
     parts = pl.pallas_call(
         attend,
@@ -185,7 +214,7 @@
         scratch_shapes=[pltpu.VMEM((n_req + 1, 8, HEAD), F32)] * 3,
         compiler_params=limit,
         name="attend",
-    )(page_owner, page_fill, got, key_pages, value_pages)
+    )(page_owner, page_fill, got, key_pages, values)
     parts = lax.all_to_all(parts, (z, w), 0, 0, tiled=True)
     columns = pl.pallas_call(
         project,

time: 84.4 us -> 76.7 us (0.909)
  Pallas kernels: 10.2 us -> 4.71 us
  local copies, waits for them, and re-layouts: 2.75 us -> 0.67 us
    pallas_call x1, Pallas kernels: 8.57 us -> 1.85 us  [on_device(): pl.pallas_call(attend, out_shape=jax.ShapeDtypeStruct((n_inst, 8, HEAD),...]
    unnamed x12 -> x6, local copies, waits for them, and re-layouts: 2.75 us -> 0.67 us
    pallas_call x1, Pallas kernels: 0.11 us -> 1.39 us  [on_device(): pl.pallas_call(prepare, out_shape=[jax.ShapeDtypeStruct((n_inst, 40, HEAD...]
where the time goes in v3:
time: 76.7 us; the launch traced here: 76.5 us
  blocking collectives  70.4 us (92%)
  Pallas kernels  4.71 us (6%)
    all_to_all x1, blocking collectives, on_device(): got = lax.all_to_all(sent, (z, w), 0, 0, tiled=True)  35 us
    all_to_all x1, blocking collectives, on_device(): lax.all_to_all(columns.reshape(nw * ny, 4, HEAD), (w, y), 0, 0, tiled=True)  18.7 us
    all_to_all x1, blocking collectives, on_device(): parts = lax.all_to_all(parts, (z, w), 0, 0, tiled=True)  16.7 us
    pallas_call x1, Pallas kernels, on_device(): pl.pallas_call(attend, out_shape=jax.ShapeDtypeStruct((n_inst, 8, HEAD),...  1.85 us

profile of v3, /device:TPU:1, one launch (start us, length us, event | category | flops | bytes accessed | tf_op | source)
XLA Modules:
  0.0 76.5 jit_solution(17122626025017546038)
XLA Ops:
  0.7 0.0 copy-start
  0.7 1.4 %prepare.1 = (bf16[64,40,128]{2,1,0:T(8,128)(2,1)S(1)}, bf16[32,128,128]{2,1,0:T(8,128)(2,1)S(1)}) custom-call(s32[1]{0:T(128)S(6)} %copy.8.req_ref, bf16[1,512]{1,0:T(2,128)(2,1)} %q_hbm.1, bf16[64,512]{1,0:T(8,128)(2,1)} %bitcast.3, bf16[32,128,128]{2,1,0:T(8,128)(2,1)} %v_hbm.1), custom_call_target="tpu_custom_call" | custom-call | tf_op jit(solution)/shard_map/prepare/pallas_call | solution.py:195
  2.1 35.0 %all_to_all.15.got_ref = bf16[64,40,128]{2,1,0:T(8,128)(2,1)S(1)} all-to-all(bf16[64,40,128]{2,1,0:T(8,128)(2,1)S(1)} %get-tuple-element.7), channel_id=1, replica_groups=mesh['z'=8,'w'=8,'y'=8] {'z','w'}, dimensions={0} | all-to-all | bytes 1310720 | tf_op jit(solution)/shard_map/all_to_all | solution.py:208
  37.0 0.0 copy-start.1
  37.0 0.0 copy-start.2
  37.0 0.0 copy-done
  37.0 0.6 copy-done.1
  37.7 0.0 copy-done.2
  37.7 1.8 %attend.1 = bf16[64,8,128]{2,1,0:T(8,128)(2,1)S(1)} custom-call(s32[32]{0:T(128)S(1)} %copy-done.1, s32[32]{0:T(128)S(1)} %copy-done.2, bf16[64,40,128]{2,1,0:T(8,128)(2,1)S(1)} %all_to_all.15.got_ref, bf16[32,128,128]{2,1,0:T(8,128)(2,1)S(1)} %copy-done, bf16[32,128,128]{2,1,0:T(8,128)(2,1)S(1)} %get-tuple-element.8.v_ref), custom_call_target="tpu_custom_call" | custom-call | tf_op jit(solution)/shard_map/attend/pallas_call | solution.py:209
  39.6 16.7 %all_to_all.16.part_ref = bf16[64,8,128]{2,1,0:T(8,128)(2,1)S(1)} all-to-all(bf16[64,8,128]{2,1,0:T(8,128)(2,1)S(1)} %attend.1), channel_id=1, replica_groups=mesh['z'=8,'w'=8,'y'=8] {'z','w'}, dimensions={0} | all-to-all | bytes 262144 | tf_op jit(solution)/shard_map/all_to_all | solution.py:218
  56.3 0.8 project.1
  57.0 18.7 %all_to_all.17.part_ref = f32[64,4,128]{2,1,0:T(4,128)S(1)} all-to-all(f32[64,4,128]{2,1,0:T(4,128)S(1)} %bitcast.2), channel_id=1, replica_groups=mesh['z'=8,'w'=8,'y'=8] {'w','y'}, dimensions={0} | all-to-all | bytes 262144 | tf_op jit(solution)/shard_map/all_to_all | solution.py:227
  75.7 0.7 finish.1
Async XLA Ops:
  0.7 36.4 %copy-start = (bf16[32,128,128]{2,1,0:T(8,128)(2,1)S(1)}, bf16[32,128,128]{2,1,0:T(8,128)(2,1)}, u32[]{:S(2)}) copy-start(bf16[32,128,128]{2,1,0:T(8,128)(2,1)} %k_ref.1) | copy-start | bytes 3145732
  37.0 0.7 copy-start.1
  37.0 0.7 copy-start.2
